TPU v7x, 16 devices: a whole 2x2x2 slice. The times are simulated.
16 devices in a mesh: data: 4 (over z, y), model: 4 (over x, core).
Axes of the slice: x: 2, y: 2, z: 2, core: 2. Of those that a mesh axis runs over, the one named last changes fastest.
Arguments:
- x: bfloat16 [512, 128, 640], P('data'), parts along dimension 0
- w_in: bfloat16 [640, 4, 2048], P(None, None, 'model')
- w_rec: bfloat16 [2048, 4, 2048], P(None, None, 'model')
- gate_bias: float32 [4, 2048], P(None, 'model')
- h_init: float32 [512, 2048], P('data', 'model'), parts along dimension 0
- c_init: float32 [512, 2048], P('data', 'model'), parts along dimension 0
Outputs:
- output 1: bfloat16 [512, 128, 2048], P('data', None, 'model'), parts along dimension 0
- output 2: float32 [512, 2048], P('data', 'model'), parts along dimension 0
- output 3: float32 [512, 2048], P('data', 'model'), parts along dimension 0
There are 4 independent parts. A program takes and returns all parts, laid end to end along the dimension named above; an argument that names none is the same for every part.
All inputs are finite; a program needn't handle non-finite values.
Results may differ from a plain program's by a relative error of at most 0.00728457.
Values are sent between devices in bfloat16 or wider.
A program may use at most 1 GiB of HBM per device.

v0:
```python
import jax
import jax.numpy as jnp
from jax import lax
from jax.sharding import PartitionSpec as P


def solution(mesh):
    def local_fn(x, w_in, w_rec, gate_bias, h_init, c_init):
        in_dim = w_in.shape[0]
        hidden = w_rec.shape[0]
        local_units = w_rec.shape[2]
        batch_rows = x.shape[0]
        w_in_flat = w_in.reshape(in_dim, 4 * local_units)
        w_rec_flat = w_rec.reshape(hidden, 4 * local_units)

        def step_fn(carry_in, x_step):
            h_prev, c_prev = carry_in
            h_gathered = lax.all_gather(h_prev.astype(jnp.bfloat16), "model", axis=1, tiled=True)
            gate_pre = jnp.dot(x_step, w_in_flat, preferred_element_type=jnp.float32) + jnp.dot(
                h_gathered, w_rec_flat, preferred_element_type=jnp.float32)
            gate_pre = gate_pre.reshape(batch_rows, 4, local_units) + gate_bias
            c_next = jax.nn.sigmoid(gate_pre[:, 1]) * c_prev + jax.nn.sigmoid(gate_pre[:, 0]) * jnp.tanh(gate_pre[:, 3])
            h_next = jax.nn.sigmoid(gate_pre[:, 2]) * jnp.tanh(c_next)
            return (h_next, c_next), h_next.astype(jnp.bfloat16)

        (h_last, c_last), y_steps = lax.scan(step_fn, (h_init, c_init), jnp.swapaxes(x, 0, 1))
        return jnp.swapaxes(y_steps, 0, 1), h_last, c_last

    return jax.shard_map(
        local_fn,
        mesh=mesh,
        in_specs=(P("data", None, None), P(None, None, "model"), P(None, None, "model"),
                  P(None, "model"), P("data", "model"), P("data", "model")),
        out_specs=(P("data", None, "model"), P("data", "model"), P("data", "model")),
        check_vma=False,
    )
```

profile of v0, /device:TPU:0, one launch (start us, length us, event | category | flops | bytes accessed | tf_op | source)
XLA Modules:
  0.0 1927.0 jit_solution(18308833037542262876)
XLA Ops:
  0.6 22.9 %copy.18 = bf16[128,128,640]{2,0,1:T(8,128)(2,1)} copy(bf16[128,128,640]{2,1,0:T(8,128)(2,1)} %param.8) | data formatting | bytes 41943040 | tf_op args[0]
  23.6 10.5 copy.14
  36.6 1871.7 %while.14 = (s32[]{:T(128)}, f32[128,512]{1,0:T(8,128)S(1)}, f32[128,512]{1,0:T(8,128)S(1)}, bf16[128,128,512]{2,1,0:T(8,128)(2,1)}, bf16[128,128,640]{2,1,0:T(8...) while((s32[]{:T(128)}, f32[128,512]{1,0:T(8,128)S(1)}, ...), condition=%wide.region_1.2_spmd, body=%wide.region_0.1_spmd.sunk | while | flops 1410793472 | bytes 19965020 | solution.py:26
  36.7 8.9 all_gather.4
  96.7 7.3 all_gather.4
  125.9 7.3 all_gather.4
  199.0 7.3 all_gather.4
  213.6 7.3 all_gather.4
  228.3 7.3 all_gather.4
  286.7 7.3 all_gather.4
  315.9 7.3 all_gather.4
  330.5 7.3 all_gather.4
  345.1 7.3 all_gather.4
  374.4 7.3 all_gather.4
  389.0 7.3 all_gather.4
  403.6 7.3 all_gather.4
  418.2 7.3 all_gather.4
  578.9 7.3 all_gather.4
  622.8 7.3 all_gather.4
  652.0 7.3 all_gather.4
  666.6 7.3 all_gather.4
  681.2 7.3 all_gather.4
  695.8 7.3 all_gather.4
  710.4 7.3 all_gather.4
  725.0 7.3 all_gather.4
  739.7 7.3 all_gather.4
  754.3 7.3 all_gather.4
  783.5 7.3 all_gather.4
  798.1 7.3 all_gather.4
  827.3 7.3 all_gather.4
  841.9 7.3 all_gather.4
  871.1 7.3 all_gather.4
  885.7 7.3 all_gather.4
  900.4 7.3 all_gather.4
  958.8 7.3 all_gather.4
  988.0 7.3 all_gather.4
  1017.2 7.3 all_gather.4
  1031.8 7.3 all_gather.4
  1061.1 7.3 all_gather.4
  1075.7 7.3 all_gather.4
  1148.7 7.3 all_gather.4
  1163.3 7.3 all_gather.4
  1178.0 7.3 all_gather.4
  1192.6 7.3 all_gather.4
  1324.1 7.3 all_gather.4
  1338.7 7.3 all_gather.4
  1367.9 7.3 all_gather.4
  1382.5 7.3 all_gather.4
  1397.1 7.3 all_gather.4
  1426.3 7.3 all_gather.4
  1440.9 7.3 all_gather.4
  1455.5 7.3 all_gather.4
  1528.5 7.3 all_gather.4
  1557.8 7.3 all_gather.4
  1572.4 7.3 all_gather.4
  1630.8 7.3 all_gather.4
  1660.0 7.3 all_gather.4
  1733.0 7.3 all_gather.4
  1762.3 7.3 all_gather.4
  1835.3 7.3 all_gather.4
  1849.9 7.3 all_gather.4
  1864.5 7.3 all_gather.4
  1879.1 7.3 all_gather.4
  1908.3 18.7 copy.19
  (720 shorter events, 1432.2 us)
Async XLA Ops:
  23.6 13.0 copy-start.1
  23.6 13.0 copy-start.3
  23.6 13.0 copy-start.4
  1908.3 18.7 copy-start
  1908.3 18.7 copy-start.2
where the time goes:
time: 1940 us; the launch traced here: 1930 us
  blocking collectives  934 us (48%)
  matrix products  792 us (41%)
  other arithmetic  143 us (7%)
  local copies, waits for them, and re-layouts  54.7 us (3%)
    all_gather x128, blocking collectives, step_fn(): lax.all_gather(h_prev.astype(jnp.bfloat16), 'model', axis=1, tiled=True)  934 us
    dot_general x128, matrix products, step_fn(): jnp.dot(h_gathered, w_rec_flat, preferred_element_type=jnp.float32)  597 us
    dot_general x128, matrix products, step_fn(): jnp.dot(x_step, w_in_flat, preferred_element_type=jnp.float32)  195 us
    dynamic_update_slice x128, other arithmetic, local_fn(): lax.scan(step_fn, (h_init, c_init), jnp.swapaxes(x, 0, 1))  122 us

commit v1 on v0

v1 whole, which is shorter than its diff:
```python
import functools

import jax
import jax.numpy as jnp
from jax import lax
from jax.experimental import pallas as pl
from jax.experimental.pallas import tpu as pltpu
from jax.sharding import PartitionSpec as P

MESH = pl.DeviceIdType.MESH
F32 = jnp.float32
BF16 = jnp.bfloat16
SLOTS = 4
XSLOTS = 3


def sigmoid(v):
    return 0.5 * jnp.tanh(0.5 * v) + 0.5


def recurrent_kernel(steps, rows, units, tile,
                     xp_ref, own_ref, other_ref, h0_ref, c0_ref,
                     y_ref, hl_ref, cl_ref,
                     w_ref, hbuf, c_ref, hf_ref, acc, xbuf,
                     wsem, xsem, hsend, hrecv, ylocal, ysend, yrecv, fin):
    per = units // tile
    nb = 2 * per
    me = lax.axis_index("model")
    core = me % 2
    chip = me // 2
    sib = 2 * chip + (1 - core)
    twin = 2 * (1 - chip) + core
    sibtwin = 2 * (1 - chip) + (1 - core)
    row0 = pl.multiple_of(chip * rows, rows)

    barrier = pltpu.get_barrier_semaphore()
    for peer in (sib, twin):
        pl.semaphore_signal(barrier, inc=1, device_id={"model": peer}, device_id_type=MESH)

    loads = []
    for half, src in enumerate((own_ref, other_ref)):
        for kb, blk in enumerate((me, twin, sib, sibtwin)):
            loads.append(pltpu.make_async_copy(
                src.at[:, pl.ds(pl.multiple_of(blk * units, units), units), :],
                w_ref.at[half, :, pl.ds(kb * units, units), :],
                wsem.at[half, kb]))
    for cp in loads:
        cp.start()

    def xcopy(t, slot):
        return pltpu.make_async_copy(xp_ref.at[t], xbuf.at[slot], xsem.at[slot])

    def hcopy(slot, j):
        return pltpu.make_async_remote_copy(
            src_ref=hbuf.at[slot, j], dst_ref=hbuf.at[slot, nb + j],
            send_sem=hsend.at[slot, j], recv_sem=hrecv.at[slot, j],
            device_id={"model": sib}, device_id_type=MESH)

    def ydst(t, j):
        return y_ref.at[t, pl.ds(row0, rows), pl.ds((j % per) * tile, tile)]

    def ycopy(t, slot, j):
        if j < per:
            return pltpu.make_async_copy(hbuf.at[slot, j], ydst(t, j), ylocal.at[slot, j])
        return pltpu.make_async_remote_copy(
            src_ref=hbuf.at[slot, j], dst_ref=ydst(t, j),
            send_sem=ysend.at[slot, j - per], recv_sem=yrecv,
            device_id={"model": twin}, device_id_type=MESH)

    def wait_y(slot, j):
        if j < per:
            ycopy(0, slot, j).wait()
        else:
            ycopy(0, slot, j).wait_send()

    for t in range(XSLOTS):
        xcopy(t, t).start()
    c_ref[...] = c0_ref[...]
    for j in range(nb):
        hbuf[0, j] = h0_ref[:, j * tile:(j + 1) * tile]

    pl.semaphore_wait(barrier, 2)
    for j in range(nb):
        hcopy(0, j).start()
    for cp in loads:
        cp.wait()

    def part_own(slot, xslot):
        h = [hbuf[slot, kb] for kb in range(nb)]
        for j in range(nb):
            half, nn = divmod(j, per)
            for k in range(4):
                s = None
                for kb in range(nb):
                    d = jnp.dot(h[kb], w_ref[half, k, kb * tile:(kb + 1) * tile, nn * tile:(nn + 1) * tile],
                                preferred_element_type=F32)
                    s = d if s is None else s + d
                col = (half * 4 + k) * units + nn * tile
                acc[j, k] = s + xbuf[xslot, :, pl.ds(col, tile)]

    def part_rest(t, slot, nslot, last):
        h = [hbuf[slot, nb + kb] for kb in range(nb)]
        for j in range(nb):
            half, nn = divmod(j, per)
            g = []
            for k in range(4):
                s = None
                for kb in range(nb):
                    row = (nb + kb) * tile
                    d = jnp.dot(h[kb], w_ref[half, k, row:row + tile, nn * tile:(nn + 1) * tile],
                                preferred_element_type=F32)
                    s = d if s is None else s + d
                g.append(s + acc[j, k])
            c = sigmoid(g[1]) * c_ref[j] + sigmoid(g[0]) * jnp.tanh(g[3])
            c_ref[j] = c
            hv = sigmoid(g[2]) * jnp.tanh(c)
            hbuf[nslot, j] = hv.astype(BF16)
            if last:
                hf_ref[j] = hv
            else:
                hcopy(nslot, j).start()
            ycopy(t, nslot, j).start()

    xcopy(0, 0).wait()
    part_own(0, 0)

    def step(t, carry):
        slot = lax.rem(t, SLOTS)
        nslot = lax.rem(t + 1, SLOTS)

        @pl.when(t >= SLOTS)
        def _():
            for j in range(nb):
                hcopy(nslot, j).wait_send()
                wait_y(nslot, j)

        @pl.when(jnp.logical_and(t >= SLOTS - 1, t < SLOTS))
        def _():
            for j in range(nb):
                hcopy(nslot, j).wait_send()

        @pl.when(t + XSLOTS < steps)
        def _():
            xcopy(t + XSLOTS, lax.rem(t, XSLOTS)).start()
        xslot = lax.rem(t + 1, XSLOTS)
        xcopy(0, xslot).wait()
        for j in range(nb):
            hcopy(slot, j).wait_recv()
        part_rest(t, slot, nslot, False)
        part_own(nslot, xslot)
        return carry

    lax.fori_loop(0, steps - 1, step, 0)

    t = steps - 1
    slot, nslot = t % SLOTS, (t + 1) % SLOTS
    for j in range(nb):
        hcopy(nslot, j).wait_send()
        wait_y(nslot, j)
        hcopy(slot, j).wait_recv()
    part_rest(t, slot, nslot, True)

    ends = []
    for n, (src, dst) in enumerate(((hf_ref, hl_ref), (c_ref, cl_ref))):
        for j in range(nb):
            d = dst.at[pl.ds(row0, rows), pl.ds((j % per) * tile, tile)]
            if j < per:
                cp = pltpu.make_async_copy(src.at[j], d, fin.at[0, n, j])
            else:
                cp = pltpu.make_async_remote_copy(
                    src_ref=src.at[j], dst_ref=d,
                    send_sem=fin.at[0, n, j], recv_sem=fin.at[1, n, j],
                    device_id={"model": twin}, device_id_type=MESH)
            cp.start()
            ends.append(cp)
    for s in range(1, SLOTS):
        q = (nslot + s) % SLOTS
        for j in range(nb):
            hcopy(q, j).wait_send()
            wait_y(q, j)
    for j in range(nb):
        wait_y(nslot, j)
    theirs = y_ref.at[:, pl.ds(pl.multiple_of((1 - chip) * rows, rows), rows), :]
    pltpu.make_async_copy(theirs, theirs, yrecv).wait()
    for cp in ends:
        cp.wait()


def recurrent(xp, own, other, h0, c0, batch, tile=256):
    steps, rows, _ = xp.shape
    units = own.shape[2]
    hidden = own.shape[1]
    nb = 2 * (units // tile)
    any_spec = pl.BlockSpec(memory_space=pl.ANY)
    vmem = pl.BlockSpec(memory_space=pltpu.VMEM)
    return pl.pallas_call(
        functools.partial(recurrent_kernel, steps, rows, units, tile),
        out_shape=(jax.ShapeDtypeStruct((steps, batch, units), BF16),
                   jax.ShapeDtypeStruct((batch, units), F32),
                   jax.ShapeDtypeStruct((batch, units), F32)),
        in_specs=[any_spec, any_spec, any_spec, vmem, vmem],
        out_specs=(any_spec, any_spec, any_spec),
        scratch_shapes=[
            pltpu.VMEM((2, 4, hidden, units), BF16),
            pltpu.VMEM((SLOTS, 2 * nb, rows, tile), BF16),
            pltpu.VMEM((nb, rows, tile), F32),
            pltpu.VMEM((nb, rows, tile), F32),
            pltpu.VMEM((nb, 4, rows, tile), F32),
            pltpu.VMEM((XSLOTS, rows, 8 * units), F32),
            pltpu.SemaphoreType.DMA((2, 4)),
            pltpu.SemaphoreType.DMA((XSLOTS,)),
            pltpu.SemaphoreType.DMA((SLOTS, nb)),
            pltpu.SemaphoreType.DMA((SLOTS, nb)),
            pltpu.SemaphoreType.DMA((SLOTS, nb // 2)),
            pltpu.SemaphoreType.DMA((SLOTS, nb // 2)),
            pltpu.SemaphoreType.DMA,
            pltpu.SemaphoreType.DMA((2, 2, nb)),
        ],
        compiler_params=pltpu.CompilerParams(
            collective_id=0, has_side_effects=True, vmem_limit_bytes=60 * 1024 * 1024),
        name="recurrent",
    )(xp, own, other, h0, c0)


def solution(mesh):
    n_model = mesh.shape["model"]
    swap = [(i, (i + n_model // 2) % n_model) for i in range(n_model)]

    def local_fn(x, w_in, w_rec, gate_bias, h_init, c_init):
        in_dim = w_in.shape[0]
        hidden, _, units = w_rec.shape
        batch, steps, _ = x.shape
        rows = batch // 2
        tile = 256
        nb = 2 * (units // tile)
        data = lax.axis_index("data")
        chip = lax.axis_index("model") // 2
        row0 = chip * rows
        orow0 = (1 - chip) * rows

        w4 = jnp.concatenate([w_rec.swapaxes(0, 1), w_in.swapaxes(0, 1)], axis=1)
        quarter = lax.dynamic_index_in_dim(w4, data, 0, keepdims=False)
        o4 = lax.all_gather(lax.ppermute(quarter, "model", swap), "data", axis=0)

        small = jnp.concatenate([
            lax.dynamic_slice_in_dim(c_init, orow0, rows, 0),
            lax.dynamic_slice_in_dim(h_init, orow0, rows, 0),
            gate_bias], axis=0)
        small_o = lax.ppermute(small, "model", swap)
        c_own = lax.dynamic_slice_in_dim(c_init, row0, rows, 0)
        h_own = lax.dynamic_slice_in_dim(h_init, row0, rows, 0)
        c0 = jnp.concatenate([c_own, small_o[:rows]], axis=1).reshape(rows, nb, tile).swapaxes(0, 1)
        h0 = jnp.concatenate([h_own, small_o[rows:2 * rows]], axis=1).astype(BF16)
        bias = jnp.concatenate([gate_bias.reshape(-1), small_o[2 * rows:].reshape(-1)])

        wx = jnp.concatenate([w4[:, hidden:], o4[:, hidden:]], axis=0)
        xt = lax.dynamic_slice_in_dim(x, row0, rows, 0).swapaxes(0, 1)
        xp = jnp.einsum("trd,gdu->trgu", xt, wx, preferred_element_type=F32)
        xp = xp.reshape(steps, rows, 8 * units) + bias

        y, h_last, c_last = recurrent(xp, w4[:, :hidden], o4[:, :hidden], h0, c0, batch, tile)
        return y.swapaxes(0, 1), h_last, c_last

    return jax.shard_map(
        local_fn,
        mesh=mesh,
        in_specs=(P("data", None, None), P(None, None, "model"), P(None, None, "model"),
                  P(None, "model"), P("data", "model"), P("data", "model")),
        out_specs=(P("data", None, "model"), P("data", "model"), P("data", "model")),
        check_vma=False,
    )
```

time: 1940 us -> 1110 us (0.57)
  blocking collectives: 934 us -> 0 us
  matrix products: 792 us -> 60.5 us
  Pallas kernels: 0 us -> 479 us
  local copies, waits for them, and re-layouts: 54.7 us -> 291 us
  waiting for transfers between devices: 0 us -> 163 us
  other arithmetic: 143 us -> 90.1 us
    all_gather x128 -> x0, blocking collectives: 934 us -> none  [step_fn(): lax.all_gather(h_prev.astype(jnp.bfloat16), 'model', axis=1, tiled=True)]
    dot_general x256 -> x1, matrix products: 792 us -> 60.5 us  [local_fn(): xp = jnp.einsum('trd,gdu->trgu', xt, wx, preferred_element_type=F32)]
    pallas_call x0 -> x1, Pallas kernels: none -> 479 us  [recurrent(): pl.pallas_call(functools.partial(recurrent_kernel, steps, rows, units, ti...]
    reshape x0 -> x2, local copies, waits for them, and re-layouts: none -> 143 us  [the longest x1 142 us: local_fn(): xp = xp.reshape(steps, rows, 8 * units) + bias]
    dynamic_update_slice x128 -> x0, other arithmetic: 122 us -> none  [local_fn(): lax.scan(step_fn, (h_init, c_init), jnp.swapaxes(x, 0, 1))]
    dot_general x0 -> x1, local copies, waits for them, and re-layouts: none -> 109 us  [local_fn(): xp = jnp.einsum('trd,gdu->trgu', xt, wx, preferred_element_type=F32)]
    all_gather x0 -> x1, waiting for transfers between devices: none -> 96.9 us  [local_fn(): o4 = lax.all_gather(lax.ppermute(quarter, 'model', swap), 'data', axis=0)]
    add x128 -> x1, other arithmetic: 18.8 us -> 87 us  [local_fn(): xp = xp.reshape(steps, rows, 8 * units) + bias]
  transfers between devices with their start and end apart: 0 -> 3, of which waited for: 0 -> 3; matrix products, arithmetic and copies ran while one was open for 0% -> 0% of each run, Pallas kernels for 0% -> 0%
where the time goes in v1:
time: 1110 us; the launch traced here: 1100 us
  Pallas kernels  479 us (43%)
  local copies, waits for them, and re-layouts  291 us (26%)
  waiting for transfers between devices  163 us (15%)
  other arithmetic  90.1 us (8%)
  matrix products  60.5 us (5%)
  between operations  14.2 us (1%)
    pallas_call x1, Pallas kernels, recurrent(): pl.pallas_call(functools.partial(recurrent_kernel, steps, rows, units, ti...  479 us
    reshape x1, local copies, waits for them, and re-layouts, local_fn(): xp = xp.reshape(steps, rows, 8 * units) + bias  142 us
    dot_general x1, local copies, waits for them, and re-layouts, local_fn(): xp = jnp.einsum('trd,gdu->trgu', xt, wx, preferred_element_type=F32)  109 us
    all_gather x1, waiting for transfers between devices, local_fn(): o4 = lax.all_gather(lax.ppermute(quarter, 'model', swap), 'data', axis=0)  96.9 us
    add x1, other arithmetic, local_fn(): xp = xp.reshape(steps, rows, 8 * units) + bias  87 us
    dot_general x1, matrix products, local_fn(): xp = jnp.einsum('trd,gdu->trgu', xt, wx, preferred_element_type=F32)  60.5 us
    ppermute x1, waiting for transfers between devices, local_fn(): o4 = lax.all_gather(lax.ppermute(quarter, 'model', swap), 'data', axis=0)  59.7 us
    unnamed x20, local copies, waits for them, and re-layouts  30.8 us
  transfers between devices with their start and end apart: 3, of which 3 were waited for; matrix products, arithmetic and copies ran while one was open for 0% of the time, Pallas kernels for 0%

profile of v1, /device:TPU:0, one launch (start us, length us, event | category | flops | bytes accessed | tf_op | source)
XLA Modules:
  0.0 1103.4 jit_solution(6775880030504762864)
XLA Ops:
  7.2 0.0 all-gather.3.cloned.1.call-start
  7.2 2.3 copy.26
  9.5 8.5 copy.25
  18.0 0.0 copy-start
  18.0 0.0 copy-start.3
  18.0 0.0 copy-start.5
  18.0 1.8 fusion.6
  19.8 3.3 collective-permute-start
  23.1 59.7 %collective-permute-done = bf16[2688,512]{1,0:T(8,128)(2,1)} collective-permute-done((bf16[2688,512]{1,0:T(8,128)(2,1)S(1)}, bf16[2688,512]{1,0:T(8,128)(2,1)}, u32[]{:S(2)}, u32[]{:S(2)}) %collective-permute-start) | collective-permute-done | bytes 2752544 | tf_op jit(solution)/shard_map/ppermute | solution.py:243
  82.7 0.0 all-gather.3.cloned.1.call-update
  82.8 0.0 copy-done
  82.8 0.0 copy-done.3
  82.8 0.0 copy-done.5
  82.9 1.8 collective-permute-start.1
  84.7 6.2 collective-permute-done.1
  90.9 0.7 copy.27
  91.6 0.6 pad_maximum_fusion.3
  92.2 0.7 pad_maximum_fusion.2.h0_ref
  92.9 96.9 %all-gather.3.cloned.1.call-done = bf16[10752,512]{1,0:T(8,128)(2,1)} async-done(((bf16[2688,512]{1,0:T(8,128)(2,1)}), bf16[10752,512]{1,0:T(8,128)(2,1)}) %all-gather.3.cloned.1.call-update) | async-done | bytes 11010064 | tf_op jit(solution)/shard_map/all_gather | solution.py:243
  189.8 1.9 slice.21
  191.7 7.1 slice.23.other_ref
  198.8 60.5 %fusion = f32[128,64,8,512]{3,0,2,1:T(8,128)} fusion(bf16[128,128,640]{2,1,0:T(8,128)(2,1)} %param.6, s32[]{:T(128)S(6)} %select_n.19, bf16[4,640,512]{2,1,0:T(8,128)(2,1)S(1)} %slice.21, bf16[4,640,512]{2,1,0:T(8,128)(2,1)S(1)} %bitcast.46), kind=kOutput, calls=%fused_computation.3 | convolution fusion | flops 42960158720 | bytes 149946368 | tf_op jit(solution)/shard_map/trd,gdu->trgu/dot_general | solution.py:258
  259.3 108.8 %copy.15 = f32[128,64,8,512]{3,2,1,0:T(8,128)} copy(f32[128,64,8,512]{3,0,2,1:T(8,128)} %fusion) | data formatting | bytes 268435456 | tf_op jit(solution)/shard_map/trd,gdu->trgu/dot_general | solution.py:258
  368.1 0.0 copy-start.4
  368.1 141.9 %reshape.19 = f32[128,64,4096]{2,1,0:T(8,128)} reshape(f32[128,64,8,512]{3,2,1,0:T(8,128)} %copy.15) | data formatting | bytes 268435456 | tf_op jit(solution)/shard_map/reshape | solution.py:259
  510.0 0.0 copy-done.4
  510.1 87.0 %broadcast_add_fusion.xp_ref = f32[128,64,4096]{2,1,0:T(8,128)} fusion(f32[128,64,4096]{2,1,0:T(8,128)} %reshape.19, f32[4096]{0:T(1024)S(1)} %copy-done.4), kind=kLoop, calls=%fused_computation | loop fusion | flops 33554432 | bytes 268451840 | tf_op jit(solution)/shard_map/add | solution.py:259
  597.1 479.4 %recurrent.1 = (bf16[128,128,512]{2,1,0:T(8,128)(2,1)}, f32[128,512]{1,0:T(8,128)}, f32[128,512]{1,0:T(8,128)}) custom-call(f32[128,64,4096]{2,1,0:T(8,128)} %broadcast_add_fusion.xp_ref, bf16[4,2048,512]{2,1,0:T(8,128)(2,1)} %bitcast.41, bf16[4,2048,512]{2,1,0:T(8,128)(2,1)} %slice.23.other_ref, bf16[64,1024]{1,0:T(8,128)(2,1)} %pad_maximum_fusion.2.h0_ref, ...), custom_call_target="tpu_custom_call" | custom-call | tf_op jit(solution)/shard_map/recurrent/pallas_call | solution.py:196
  1076.5 0.0 copy-start.2
  1076.5 0.0 copy-start.1
  1076.5 18.6 %copy.17 = bf16[128,128,512]{2,1,0:T(8,128)(2,1)} copy(bf16[128,128,512]{2,0,1:T(8,128)(2,1)} %bitcast.42) | data formatting | bytes 33554432
  1095.1 0.0 copy-done.2
  1095.1 0.7 copy.30
  1095.8 0.0 copy-done.1
  1095.8 0.7 copy.31
  (9 shorter events, 0.1 us)
Async XLA Ops:
  7.2 182.6 %all-gather.3.cloned.1.call-start = ((), (), s32[]{:S(2)}) async-start(), calls=%async_computation | async-start | bytes 13762560 | tf_op jit(solution)/shard_map/all_gather | solution.py:243
  18.0 64.8 %copy-start = (f32[128,512]{1,0:T(8,128)S(1)}, f32[128,512]{1,0:T(8,128)}, u32[]{:S(2)}) copy-start(f32[128,512]{1,0:T(8,128)} %param.11) | copy-start | bytes 786436
  18.0 64.8 %copy-start.3 = (f32[128,512]{1,0:T(8,128)S(1)}, f32[128,512]{1,0:T(8,128)}, u32[]{:S(2)}) copy-start(f32[128,512]{1,0:T(8,128)} %param.10) | copy-start | bytes 786436
  18.0 64.9 %copy-start.5 = (f32[4,512]{1,0:T(4,128)S(1)}, f32[4,512]{1,0:T(4,128)}, u32[]{:S(2)}) copy-start(f32[4,512]{1,0:T(4,128)} %param.9) | copy-start | bytes 24580
  19.8 62.9 %collective-permute-start = (bf16[2688,512]{1,0:T(8,128)(2,1)S(1)}, bf16[2688,512]{1,0:T(8,128)(2,1)}, u32[]{:S(2)}, u32[]{:S(2)}) collective-permute-start(bf16[2688,512]{1,0:T(8,128)(2,1)S(1)} %fusion.6), channel_id=1, source_target_pairs={{0,2},{1,3},{2,0},{3,1},{4,6},{5,7},{6,4},{7,5},{8,10},{9,11},{10,... | collective-permute-start | bytes 8257544 | tf_op jit(solution)/shard_map/ppermute | solution.py:243
  82.9 8.0 collective-permute-start.1
  368.1 141.9 %copy-start.4 = (f32[4096]{0:T(1024)S(1)}, f32[4096]{0:T(1024)}, u32[]{:S(2)}) copy-start(f32[4096]{0:T(1024)} %pad_maximum_fusion.3) | copy-start | bytes 49156
  1076.5 18.6 %copy-start.2 = (f32[128,512]{1,0:T(8,128)S(1)}, f32[128,512]{1,0:T(8,128)}, u32[]{:S(2)}) copy-start(f32[128,512]{1,0:T(8,128)} %get-tuple-element.22) | copy-start | bytes 786436
  1076.5 19.3 %copy-start.1 = (f32[128,512]{1,0:T(8,128)S(1)}, f32[128,512]{1,0:T(8,128)}, u32[]{:S(2)}) copy-start(f32[128,512]{1,0:T(8,128)} %get-tuple-element.23) | copy-start | bytes 786436
Sparse Core Ops, SparseCore 0:
  82.9 106.8 all-gather.2

commit v2 on v0

v2 whole, which is shorter than its diff:
```python
import jax
import jax.numpy as jnp
from jax import lax
from jax.experimental import pallas as pl
from jax.experimental.pallas import tpu as pltpu
from jax.sharding import PartitionSpec as P

MESH = pl.DeviceIdType.MESH
F32 = jnp.float32
BF16 = jnp.bfloat16
SLOTS = 4
XSLOTS = 3
TC = 8
CH = 128


def sigmoid(v):
    return 0.5 * jnp.tanh(0.5 * v) + 0.5


def lstm_kernel(steps, rows, units, tile, in_dim,
                xt_ref, wx_ref, wh_ref, bias_ref, h0_ref, c0_ref,
                y_ref, hl_ref, cl_ref, xp_ref,
                w_ref, hbuf, c_ref, hf_ref, acc, xbuf, bias_v, xin, xout,
                wsem, isem, rsem, ssem, insem, outsem,
                xsem, hsend, hrecv, ylocal, ysend, yrecv, fin):
    per = units // tile
    nb = 2 * per
    me = lax.axis_index("model")
    data = lax.axis_index("data")
    core = me % 2
    chip = me // 2
    sib = 2 * chip + (1 - core)
    twin = 2 * (1 - chip) + core
    sibtwin = 2 * (1 - chip) + (1 - core)
    ynbr = 2 * (data // 2) + (1 - data % 2)
    znbr = 2 * (1 - data // 2) + data % 2
    diag = 2 * (1 - data // 2) + (1 - data % 2)
    row0 = pl.multiple_of(chip * rows, rows)
    orow0 = pl.multiple_of((1 - chip) * rows, rows)

    hbuf[...] = jnp.zeros(hbuf.shape, BF16)
    barrier = pltpu.get_barrier_semaphore()
    for peer in ({"model": sib}, {"model": twin}, {"data": ynbr}, {"data": znbr}):
        pl.semaphore_signal(barrier, inc=1, device_id=peer, device_id_type=MESH)

    loads = [pltpu.make_async_copy(wx_ref, w_ref.at[0, :, pl.ds(0, in_dim), :], wsem.at[0])]
    for kb, blk in enumerate((me, twin, sib, sibtwin)):
        loads.append(pltpu.make_async_copy(
            wh_ref.at[:, pl.ds(pl.multiple_of(blk * units, units), units), :],
            w_ref.at[0, :, pl.ds(in_dim + kb * units, units), :],
            wsem.at[1 + kb]))
    for cp in loads:
        cp.start()

    def xin_copy(c, slot):
        return pltpu.make_async_copy(
            xt_ref.at[pl.ds(c * TC, TC)], xin.at[slot], insem.at[slot])

    xin_copy(0, 0).start()
    own_init = [pltpu.make_async_copy(bias_ref, bias_v.at[0], isem.at[0, 0])]
    for n in range(per):
        cols = pl.ds(n * tile, tile)
        own_init.append(pltpu.make_async_copy(h0_ref.at[pl.ds(row0, rows), cols], hf_ref.at[n], isem.at[0, 1 + n]))
        own_init.append(pltpu.make_async_copy(c0_ref.at[pl.ds(row0, rows), cols], c_ref.at[n], isem.at[0, 1 + per + n]))
    for cp in own_init:
        cp.start()

    pl.semaphore_wait(barrier, 4)

    n_chunks = (in_dim + 4 * units) // CH

    def landing(g, s):
        return w_ref.at[1, g, pl.ds(pl.multiple_of(s * CH, CH), CH), :]

    def from_twin(rel, g, s):
        if s * CH < in_dim:
            src = wx_ref.at[g, pl.ds(s * CH, CH), :]
        else:
            kb, off = divmod(s * CH - in_dim, units)
            blk = (twin, me, sibtwin, sib)[kb]
            src = wh_ref.at[g, pl.ds(pl.multiple_of(blk * units + off, CH), CH), :]
        return pltpu.make_async_remote_copy(
            src_ref=src, dst_ref=landing(g, s),
            send_sem=ssem.at[0 if rel == 0 else 1, s], recv_sem=rsem.at[rel, s],
            device_id={"model": twin}, device_id_type=MESH)

    def relay(peer, link, rel, g, s):
        return pltpu.make_async_remote_copy(
            src_ref=landing(g, s), dst_ref=landing(g, s),
            send_sem=ssem.at[link, s], recv_sem=rsem.at[rel, s],
            device_id={"data": peer}, device_id_type=MESH)

    other_init = [pltpu.make_async_remote_copy(
        src_ref=bias_ref, dst_ref=bias_v.at[1], send_sem=isem.at[1, 0], recv_sem=isem.at[2, 0],
        device_id={"model": twin}, device_id_type=MESH)]
    for n in range(per):
        cols = pl.ds(n * tile, tile)
        for src, dst, at in ((h0_ref, hf_ref, 1), (c0_ref, c_ref, 1 + per)):
            other_init.append(pltpu.make_async_remote_copy(
                src_ref=src.at[pl.ds(orow0, rows), cols], dst_ref=dst.at[per + n],
                send_sem=isem.at[1, at + n], recv_sem=isem.at[2, at + n],
                device_id={"model": twin}, device_id_type=MESH))
    for s in range(n_chunks):
        from_twin(0, data, s).start()
        if s % 3 == 0:
            from_twin(3, diag, s).start()
        if s == 4:
            for cp in other_init:
                cp.start()

    def forward(s):
        relay(ynbr, 2, 0, data, s).wait_recv()
        relay(ynbr, 2, 1, data, s).start()
        relay(znbr, 3, 2, data, s).start()

    def forward_diag(s):
        relay(ynbr, 2, 1, data, s).wait_recv()
        relay(znbr, 3, 2, data, s).wait_recv()

        @pl.when(lax.rem(s, 3) == 1)
        def _():
            relay(ynbr, 4, 3, znbr, s).start()

        @pl.when(lax.rem(s, 3) == 2)
        def _():
            relay(znbr, 5, 3, ynbr, s).start()

    def xout_copy(half, c, slot):
        return pltpu.make_async_copy(
            xout.at[slot], xp_ref.at[pl.ds(c * TC, TC), pl.ds(half * 4 * per, 4 * per)], outsem.at[slot])

    def project(it, carry):
        half = it // (steps // TC)
        c = lax.rem(it, steps // TC)
        slot = lax.rem(it, 2)

        @pl.when(slot == 0)
        def _():
            s = it // 2
            forward(s)

            @pl.when(s >= 1)
            def _():
                forward_diag(s - 1)

        @pl.when(it == steps // TC)
        def _():
            for s in range(in_dim // CH):
                relay(ynbr, 4, 3, diag, s).wait_recv()
            other_init[0].wait_recv()

        xin_copy(c, slot).wait()

        @pl.when(it + 1 < 2 * (steps // TC))
        def _():
            xin_copy(lax.rem(it + 1, steps // TC), 1 - slot).start()

        @pl.when(it >= 2)
        def _():
            xout_copy(half, c, slot).wait()

        xv = xin[slot].reshape(TC * rows, in_dim)
        for k in range(4):
            for nn in range(per):
                cols = slice(nn * tile, (nn + 1) * tile)
                g = jnp.dot(xv, w_ref[half, k, 0:in_dim, cols], preferred_element_type=F32)
                xout[slot, :, k * per + nn] = (g + bias_v[half, k:k + 1, cols]).reshape(TC, rows, tile)
        xout_copy(half, c, slot).start()
        return carry

    for cp in own_init + loads:
        cp.wait()
    n_proj = 2 * (steps // TC)
    lax.fori_loop(0, n_proj, project, 0)
    for slot in range(2):
        xout_copy(0, 0, slot).wait()

    def xcopy(t, slot):
        return pltpu.make_async_copy(xp_ref.at[t], xbuf.at[slot], xsem.at[slot])

    for t in range(XSLOTS):
        xcopy(t, t).start()

    def tail(s, carry):
        forward(s)
        forward_diag(s - 1)
        return carry

    lax.fori_loop(n_proj // 2, n_chunks, tail, 0)
    forward_diag(n_chunks - 1)

    def hcopy(slot):
        return pltpu.make_async_remote_copy(
            src_ref=hbuf.at[slot, 0, pl.ds(0, rows)], dst_ref=hbuf.at[slot, 1, pl.ds(0, rows)],
            send_sem=hsend.at[slot], recv_sem=hrecv.at[slot],
            device_id={"model": sib}, device_id_type=MESH)

    def ylocal_copy(t, slot):
        return pltpu.make_async_copy(
            hbuf.at[slot, 0, pl.ds(0, rows), pl.ds(0, units)], y_ref.at[t, pl.ds(row0, rows)], ylocal.at[slot])

    def ytwin_copy(t, slot):
        return pltpu.make_async_remote_copy(
            src_ref=hbuf.at[slot, 0, pl.ds(0, rows), pl.ds(units, units)], dst_ref=y_ref.at[t, pl.ds(row0, rows)],
            send_sem=ysend.at[slot], recv_sem=yrecv,
            device_id={"model": twin}, device_id_type=MESH)

    def wait_y(slot):
        ylocal_copy(0, slot).wait()
        ytwin_copy(0, slot).wait_send()

    for cp in other_init[1:]:
        cp.wait_recv()
    for j in range(nb):
        hbuf[0, 0, 0:rows, j * tile:(j + 1) * tile] = hf_ref[j].astype(BF16)
    hcopy(0).start()
    for s in range(in_dim // CH, n_chunks):
        relay(ynbr, 4, 3, diag, s).wait_recv()

    deep = nb * tile
    cut = deep // 2

    def product(slot, side, j, k, lo, hi):
        half, nn = divmod(j, per)
        row = in_dim + side * deep
        w = w_ref[half, k, row + lo:row + hi, nn * tile:(nn + 1) * tile]
        return jnp.dot(hbuf[slot, side, :, lo:hi], w, preferred_element_type=F32)[:rows]

    def part_own(slot, xslot, stage):
        for j in range(nb):
            half, nn = divmod(j, per)
            for k in range(4):
                if j < nb // 2:
                    if stage == 0:
                        acc[j, k] = product(slot, 0, j, k, 0, cut) + xbuf[xslot, (half * 4 + k) * per + nn]
                    else:
                        acc[j, k] = product(slot, 0, j, k, cut, deep) + acc[j, k]
                elif stage == 1:
                    acc[j, k] = product(slot, 0, j, k, 0, deep) + xbuf[xslot, (half * 4 + k) * per + nn]

    def part_rest(slot, nslot, last):
        for j in range(nb):
            g = [product(slot, 1, j, k, 0, deep) + acc[j, k] for k in range(4)]
            c = sigmoid(g[1]) * c_ref[j] + sigmoid(g[0]) * jnp.tanh(g[3])
            c_ref[j] = c
            hv = sigmoid(g[2]) * jnp.tanh(c)
            hbuf[nslot, 0, 0:rows, j * tile:(j + 1) * tile] = hv.astype(BF16)
            if last:
                hf_ref[j] = hv

    xcopy(0, 0).wait()
    part_own(0, 0, 0)
    part_own(0, 0, 1)

    def step(t, carry):
        slot = lax.rem(t, SLOTS)
        nslot = lax.rem(t + 1, SLOTS)

        @pl.when(t >= SLOTS)
        def _():
            hcopy(nslot).wait_send()
            wait_y(nslot)

        @pl.when(t == SLOTS - 1)
        def _():
            hcopy(nslot).wait_send()

        @pl.when(t + XSLOTS < steps)
        def _():
            xcopy(t + XSLOTS, lax.rem(t, XSLOTS)).start()
        xslot = lax.rem(t + 1, XSLOTS)
        xcopy(0, xslot).wait()
        hcopy(slot).wait_recv()
        part_rest(slot, nslot, False)
        part_own(nslot, xslot, 0)
        hcopy(nslot).start()
        ylocal_copy(t, nslot).start()
        ytwin_copy(t, nslot).start()
        part_own(nslot, xslot, 1)
        return carry

    lax.fori_loop(0, steps - 1, step, 0)

    t = steps - 1
    slot, nslot = t % SLOTS, (t + 1) % SLOTS
    hcopy(nslot).wait_send()
    wait_y(nslot)
    hcopy(slot).wait_recv()
    part_rest(slot, nslot, True)
    ylocal_copy(t, nslot).start()
    ytwin_copy(t, nslot).start()

    ends = []
    for n, (src, dst) in enumerate(((hf_ref, hl_ref), (c_ref, cl_ref))):
        for j in range(nb):
            d = dst.at[pl.ds(row0, rows), pl.ds((j % per) * tile, tile)]
            if j < per:
                cp = pltpu.make_async_copy(src.at[j], d, fin.at[0, n, j])
            else:
                cp = pltpu.make_async_remote_copy(
                    src_ref=src.at[j], dst_ref=d,
                    send_sem=fin.at[0, n, j], recv_sem=fin.at[1, n, j],
                    device_id={"model": twin}, device_id_type=MESH)
            cp.start()
            ends.append(cp)
    for s in range(1, SLOTS):
        q = (nslot + s) % SLOTS
        hcopy(q).wait_send()
        wait_y(q)
    wait_y(nslot)
    theirs = y_ref.at[:, pl.ds(pl.multiple_of((1 - chip) * rows, rows), rows), :]
    pltpu.make_async_copy(theirs, theirs, yrecv).wait()
    for cp in ends:
        cp.wait()
    for cp in other_init:
        cp.wait_send()
    for s in range(n_chunks):
        from_twin(0, data, s).wait_send()
        relay(ynbr, 2, 1, data, s).wait_send()
        relay(znbr, 3, 2, data, s).wait_send()
        if s % 3 == 0:
            from_twin(3, diag, s).wait_send()
        else:
            relay(ynbr, 3 + s % 3, 3, diag, s).wait_send()


def lstm(xt, wx, wh, bias, h0, c0, tile=256):
    steps, rows, in_dim = xt.shape
    hidden, units = wh.shape[1:]
    batch = h0.shape[0]
    nb = 2 * (units // tile)
    n_chunks = (in_dim + hidden) // CH
    any_spec = pl.BlockSpec(memory_space=pl.ANY)

    def kernel(*refs):
        lstm_kernel(steps, rows, units, tile, in_dim, *refs)

    return pl.pallas_call(
        kernel,
        out_shape=(jax.ShapeDtypeStruct((steps, batch, units), BF16),
                   jax.ShapeDtypeStruct((batch, units), F32),
                   jax.ShapeDtypeStruct((batch, units), F32),
                   jax.ShapeDtypeStruct((steps, 4 * nb, rows, tile), F32)),
        in_specs=[any_spec] * 6,
        out_specs=(any_spec,) * 4,
        scratch_shapes=[
            pltpu.VMEM((2, 4, in_dim + hidden, units), BF16),
            pltpu.VMEM((SLOTS, 2, 2 * rows, nb * tile), BF16),
            pltpu.VMEM((nb, rows, tile), F32),
            pltpu.VMEM((nb, rows, tile), F32),
            pltpu.VMEM((nb, 4, rows, tile), F32),
            pltpu.VMEM((XSLOTS, 4 * nb, rows, tile), F32),
            pltpu.VMEM((2, 8, units), F32),
            pltpu.VMEM((2, TC, rows, in_dim), BF16),
            pltpu.VMEM((2, TC, 2 * nb, rows, tile), F32),
            pltpu.SemaphoreType.DMA((5,)),
            pltpu.SemaphoreType.DMA((3, 1 + nb)),
            pltpu.SemaphoreType.DMA((4, n_chunks)),
            pltpu.SemaphoreType.DMA((6, n_chunks)),
            pltpu.SemaphoreType.DMA((2,)),
            pltpu.SemaphoreType.DMA((2,)),
            pltpu.SemaphoreType.DMA((XSLOTS,)),
            pltpu.SemaphoreType.DMA((SLOTS,)),
            pltpu.SemaphoreType.DMA((SLOTS,)),
            pltpu.SemaphoreType.DMA((SLOTS,)),
            pltpu.SemaphoreType.DMA((SLOTS,)),
            pltpu.SemaphoreType.DMA,
            pltpu.SemaphoreType.DMA((2, 2, nb)),
        ],
        compiler_params=pltpu.CompilerParams(
            collective_id=0, has_side_effects=True, vmem_limit_bytes=60 * 1024 * 1024),
        name="recurrent",
    )(xt, wx, wh, bias, h0, c0)


def solution(mesh):
    def local_fn(x, w_in, w_rec, gate_bias, h_init, c_init):
        rows = x.shape[0] // 2
        row0 = (lax.axis_index("model") // 2) * rows
        xt = lax.dynamic_slice_in_dim(x, row0, rows, 0).swapaxes(0, 1)
        bias = jnp.pad(gate_bias, ((0, 4), (0, 0)))
        y, h_last, c_last, _ = lstm(xt, w_in.swapaxes(0, 1), w_rec.swapaxes(0, 1), bias, h_init, c_init)
        return y.swapaxes(0, 1), h_last, c_last

    return jax.shard_map(
        local_fn,
        mesh=mesh,
        in_specs=(P("data", None, None), P(None, None, "model"), P(None, None, "model"),
                  P(None, "model"), P("data", "model"), P("data", "model")),
        out_specs=(P("data", None, "model"), P("data", "model"), P("data", "model")),
        check_vma=False,
    )
```

time: 1940 us -> 491 us (0.25)
  blocking collectives: 934 us -> 0 us
  matrix products: 792 us -> 0 us
  Pallas kernels: 0 us -> 432 us
  other arithmetic: 143 us -> 0 us
    all_gather x128 -> x0, blocking collectives: 934 us -> none  [step_fn(): lax.all_gather(h_prev.astype(jnp.bfloat16), 'model', axis=1, tiled=True)]
    dot_general x256 -> x0, matrix products: 792 us -> none  [the longest x128 597 us: step_fn(): jnp.dot(h_gathered, w_rec_flat, preferred_element_type=jnp.float32)]
    pallas_call x0 -> x1, Pallas kernels: none -> 432 us  [lstm(): pl.pallas_call(kernel, out_shape=(jax.ShapeDtypeStruct((steps, batch, uni...]
    dynamic_update_slice x128 -> x0, other arithmetic: 122 us -> none  [local_fn(): lax.scan(step_fn, (h_init, c_init), jnp.swapaxes(x, 0, 1))]
    unnamed x13 -> x10, local copies, waits for them, and re-layouts: 36 us -> 46.1 us
where the time goes in v2:
time: 491 us; the launch traced here: 490 us
  Pallas kernels  432 us (88%)
  local copies, waits for them, and re-layouts  57.2 us (12%)
    pallas_call x1, Pallas kernels, lstm(): pl.pallas_call(kernel, out_shape=(jax.ShapeDtypeStruct((steps, batch, uni...  432 us
    unnamed x10, local copies, waits for them, and re-layouts  46.1 us

profile of v2, /device:TPU:0, one launch (start us, length us, event | category | flops | bytes accessed | tf_op | source)
XLA Modules:
  0.0 490.3 jit_solution(10214501056966975693)
XLA Ops:
  0.6 1.3 pad.4.refs_3_
  2.0 3.8 copy.19
  5.7 8.3 %copy.18 = bf16[2048,4,512]{2,0,1:T(8,128)(2,1)} copy(bf16[2048,4,512]{2,1,0:T(4,128)(2,1)} %param.8) | data formatting | bytes 16777216 | tf_op args[2]
  14.1 9.8 %constant_dynamic-slice_fusion = bf16[64,128,640]{2,1,0:T(8,128)(2,1)} fusion(bf16[128,128,640]{2,1,0:T(8,128)(2,1)} %param.6, s32[]{:T(128)S(6)} %select_n.9), kind=kLoop, calls=%fused_computation.3 | loop fusion | bytes 20971524 | tf_op jit(solution)/shard_map/dynamic_slice | solution.py:381
  23.8 14.0 %copy.17 = bf16[64,128,640]{2,0,1:T(8,128)(2,1)} copy(bf16[64,128,640]{2,1,0:T(8,128)(2,1)} %constant_dynamic-slice_fusion) | data formatting | bytes 20971520
  37.9 432.4 %recurrent.1 = (bf16[128,128,512]{2,1,0:T(8,128)(2,1)}, f32[128,512]{1,0:T(8,128)}, f32[128,512]{1,0:T(8,128)}, f32[128,16,64,256]{3,2,1,0:T(8,128)}) custom-call(bf16[128,64,640]{2,1,0:T(8,128)(2,1)} %bitcast.10, bf16[4,640,512]{2,1,0:T(8,128)(2,1)} %bitcast.13, bf16[4,2048,512]{2,1,0:T(8,128)(2,1)} %bitcast.11, f32[8,512]{1,0:T(8,128)} %pad.4.refs_3_, ...), custom_call_target="tpu_custom_call" | custom-call | tf_op jit(solution)/shard_map/recurrent/pallas_call | solution.py:339
  470.2 0.0 copy-start.1
  470.2 0.0 copy-start
  470.3 18.6 %copy.12 = bf16[128,128,512]{2,1,0:T(8,128)(2,1)} copy(bf16[128,128,512]{2,0,1:T(8,128)(2,1)} %bitcast.12) | data formatting | bytes 33554432
  488.8 0.0 copy-done.1
  488.9 0.7 copy.22
  489.6 0.0 copy-done
  489.6 0.7 copy.23
Async XLA Ops:
  470.2 18.6 %copy-start.1 = (f32[128,512]{1,0:T(8,128)S(1)}, f32[128,512]{1,0:T(8,128)}, u32[]{:S(2)}) copy-start(f32[128,512]{1,0:T(8,128)} %get-tuple-element.16) | copy-start | bytes 786436
  470.2 19.3 %copy-start = (f32[128,512]{1,0:T(8,128)S(1)}, f32[128,512]{1,0:T(8,128)}, u32[]{:S(2)}) copy-start(f32[128,512]{1,0:T(8,128)} %get-tuple-element.17) | copy-start | bytes 786436

commit v3 on v2

--- a/solution.py
+++ b/solution.py
@@ -10,7 +10,11 @@
 BF16 = jnp.bfloat16
 SLOTS = 4
 XSLOTS = 3
+TX = 16
 TC = 8
+LAG = 2
+DELAY = 2
+AHEAD = 5
 CH = 128
 
 
@@ -19,9 +23,9 @@
 
 
 def lstm_kernel(steps, rows, units, tile, in_dim,
-                xt_ref, wx_ref, wh_ref, bias_ref, h0_ref, c0_ref,
+                x_ref, wx_ref, wh_ref, bias_ref, h0_ref, c0_ref,
                 y_ref, hl_ref, cl_ref, xp_ref,
-                w_ref, hbuf, c_ref, hf_ref, acc, xbuf, bias_v, xin, xout,
+                w_ref, hbuf, c_ref, hf_ref, acc, xbuf, bias_v, xraw, xf, xt, xout,
                 wsem, isem, rsem, ssem, insem, outsem,
                 xsem, hsend, hrecv, ylocal, ysend, yrecv, fin):
     per = units // tile
@@ -53,11 +57,12 @@
     for cp in loads:
         cp.start()
 
-    def xin_copy(c, slot):
+    def x_copy(n, slot):
         return pltpu.make_async_copy(
-            xt_ref.at[pl.ds(c * TC, TC)], xin.at[slot], insem.at[slot])
-
-    xin_copy(0, 0).start()
+            x_ref.at[pl.ds(row0, rows), pl.ds(pl.multiple_of(n * TX, TX), TX)], xraw.at[slot], insem.at[slot])
+
+    x_copy(0, 0).start()
+
     own_init = [pltpu.make_async_copy(bias_ref, bias_v.at[0], isem.at[0, 0])]
     for n in range(per):
         cols = pl.ds(n * tile, tile)
@@ -73,12 +78,15 @@
     def landing(g, s):
         return w_ref.at[1, g, pl.ds(pl.multiple_of(s * CH, CH), CH), :]
 
-    def from_twin(rel, g, s):
-        if s * CH < in_dim:
-            src = wx_ref.at[g, pl.ds(s * CH, CH), :]
+    wx_chunks = in_dim // CH
+
+    def from_twin(rel, g, s, of_wx):
+        if of_wx:
+            src = wx_ref.at[g, pl.ds(pl.multiple_of(s * CH, CH), CH), :]
         else:
-            kb, off = divmod(s * CH - in_dim, units)
-            blk = (twin, me, sibtwin, sib)[kb]
+            kb = (s - wx_chunks) * CH // units
+            off = (s - wx_chunks) * CH % units
+            blk = 2 * ((chip + 1 + kb) % 2) + (core + kb // 2) % 2
             src = wh_ref.at[g, pl.ds(pl.multiple_of(blk * units + off, CH), CH), :]
         return pltpu.make_async_remote_copy(
             src_ref=src, dst_ref=landing(g, s),
@@ -101,18 +109,36 @@
                 src_ref=src.at[pl.ds(orow0, rows), cols], dst_ref=dst.at[per + n],
                 send_sem=isem.at[1, at + n], recv_sem=isem.at[2, at + n],
                 device_id={"model": twin}, device_id_type=MESH))
-    for s in range(n_chunks):
-        from_twin(0, data, s).start()
+    for s in range(AHEAD):
+        from_twin(0, data, s, True).start()
         if s % 3 == 0:
-            from_twin(3, diag, s).start()
-        if s == 4:
-            for cp in other_init:
-                cp.start()
+            from_twin(3, diag, s, True).start()
+    for cp in other_init:
+        cp.start()
+    first_late = -(-wx_chunks // 3) * 3
+    n_late = len(range(first_late, n_chunks, 3))
 
     def forward(s):
         relay(ynbr, 2, 0, data, s).wait_recv()
         relay(ynbr, 2, 1, data, s).start()
         relay(znbr, 3, 2, data, s).start()
+        nxt = s + AHEAD
+
+        @pl.when(nxt < wx_chunks)
+        def _():
+            from_twin(0, data, nxt, True).start()
+
+            @pl.when(lax.rem(nxt, 3) == 0)
+            def _():
+                from_twin(3, diag, nxt, True).start()
+
+        @pl.when(jnp.logical_and(nxt >= wx_chunks, nxt < n_chunks))
+        def _():
+            from_twin(0, data, nxt, False).start()
+
+        @pl.when(s >= n_chunks - n_late)
+        def _():
+            from_twin(3, diag, first_late + 3 * (s - (n_chunks - n_late)), False).start()
 
     def forward_diag(s):
         relay(ynbr, 2, 1, data, s).wait_recv()
@@ -125,6 +151,15 @@
         @pl.when(lax.rem(s, 3) == 2)
         def _():
             relay(znbr, 5, 3, ynbr, s).start()
+
+    def stage(i):
+        @pl.when(i < n_chunks)
+        def _():
+            forward(i)
+
+        @pl.when(jnp.logical_and(i >= LAG, i < n_chunks + LAG))
+        def _():
+            forward_diag(i - LAG)
 
     def xout_copy(half, c, slot):
         return pltpu.make_async_copy(
@@ -135,14 +170,15 @@
         c = lax.rem(it, steps // TC)
         slot = lax.rem(it, 2)
 
-        @pl.when(slot == 0)
-        def _():
-            s = it // 2
-            forward(s)
-
-            @pl.when(s >= 1)
-            def _():
-                forward_diag(s - 1)
+        late = it - steps // TC
+
+        @pl.when(jnp.logical_and(it >= DELAY, late < 0))
+        def _():
+            stage(it - DELAY)
+
+        @pl.when(jnp.logical_and(late >= 0, lax.rem(late, 3) < 2))
+        def _():
+            stage(steps // TC - DELAY + late // 3 * 2 + lax.rem(late, 3))
 
         @pl.when(it == steps // TC)
         def _():
@@ -150,17 +186,29 @@
                 relay(ynbr, 4, 3, diag, s).wait_recv()
             other_init[0].wait_recv()
 
-        xin_copy(c, slot).wait()
-
-        @pl.when(it + 1 < 2 * (steps // TC))
-        def _():
-            xin_copy(lax.rem(it + 1, steps // TC), 1 - slot).start()
+        @pl.when(jnp.logical_and(slot == 0, half == 0))
+        def _():
+            n = it // 2
+            xslot = lax.rem(n, 2)
+            x_copy(n, xslot).wait()
+
+            @pl.when(n + 1 < steps // TX)
+            def _():
+                x_copy(n + 1, 1 - xslot).start()
+
+            for f in range(in_dim // 128):
+                lanes = slice(f * 128, (f + 1) * 128)
+                xf[f] = xraw[xslot, :, :, lanes].astype(F32).reshape(rows * TX, 128)
+            for f in range(in_dim // 128):
+                lanes = slice(f * 128, (f + 1) * 128)
+                for tt in range(TX):
+                    xt[n * TX + tt, :, lanes] = xf[f, pl.ds(tt, rows, stride=TX), :].astype(BF16)
 
         @pl.when(it >= 2)
         def _():
             xout_copy(half, c, slot).wait()
 
-        xv = xin[slot].reshape(TC * rows, in_dim)
+        xv = xt[pl.ds(c * TC, TC)].reshape(TC * rows, in_dim)
         for k in range(4):
             for nn in range(per):
                 cols = slice(nn * tile, (nn + 1) * tile)
@@ -182,13 +230,12 @@
     for t in range(XSLOTS):
         xcopy(t, t).start()
 
-    def tail(s, carry):
-        forward(s)
-        forward_diag(s - 1)
+    def tail(i, carry):
+        stage(i)
         return carry
 
-    lax.fori_loop(n_proj // 2, n_chunks, tail, 0)
-    forward_diag(n_chunks - 1)
+    n_stages = steps // TC - DELAY + sum(i % 3 < 2 for i in range(steps // TC))
+    lax.fori_loop(n_stages, max(n_stages, n_chunks + LAG), tail, 0)
 
     def hcopy(slot):
         return pltpu.make_async_remote_copy(
@@ -215,9 +262,6 @@
     for j in range(nb):
         hbuf[0, 0, 0:rows, j * tile:(j + 1) * tile] = hf_ref[j].astype(BF16)
     hcopy(0).start()
-    for s in range(in_dim // CH, n_chunks):
-        relay(ynbr, 4, 3, diag, s).wait_recv()
-
     deep = nb * tile
     cut = deep // 2
 
@@ -249,9 +293,14 @@
             if last:
                 hf_ref[j] = hv
 
+    own_chunks = (in_dim + deep) // CH
+    for s in range(in_dim // CH, own_chunks):
+        relay(ynbr, 4, 3, diag, s).wait_recv()
     xcopy(0, 0).wait()
     part_own(0, 0, 0)
     part_own(0, 0, 1)
+    for s in range(own_chunks, n_chunks):
+        relay(ynbr, 4, 3, diag, s).wait_recv()
 
     def step(t, carry):
         slot = lax.rem(t, SLOTS)
@@ -316,19 +365,19 @@
     for cp in other_init:
         cp.wait_send()
     for s in range(n_chunks):
-        from_twin(0, data, s).wait_send()
+        from_twin(0, data, s, s < wx_chunks).wait_send()
         relay(ynbr, 2, 1, data, s).wait_send()
         relay(znbr, 3, 2, data, s).wait_send()
         if s % 3 == 0:
-            from_twin(3, diag, s).wait_send()
+            from_twin(3, diag, s, s < wx_chunks).wait_send()
         else:
             relay(ynbr, 3 + s % 3, 3, diag, s).wait_send()
 
 
-def lstm(xt, wx, wh, bias, h0, c0, tile=256):
-    steps, rows, in_dim = xt.shape
+def lstm(x, wx, wh, bias, h0, c0, tile=256):
+    batch, steps, in_dim = x.shape
+    rows = batch // 2
     hidden, units = wh.shape[1:]
-    batch = h0.shape[0]
     nb = 2 * (units // tile)
     n_chunks = (in_dim + hidden) // CH
     any_spec = pl.BlockSpec(memory_space=pl.ANY)
@@ -351,8 +400,10 @@
             pltpu.VMEM((nb, rows, tile), F32),
             pltpu.VMEM((nb, 4, rows, tile), F32),
             pltpu.VMEM((XSLOTS, 4 * nb, rows, tile), F32),
-            pltpu.VMEM((2, 8, units), F32),
-            pltpu.VMEM((2, TC, rows, in_dim), BF16),
+            pltpu.VMEM((2, 4, units), F32),
+            pltpu.VMEM((2, rows, TX, in_dim), BF16),
+            pltpu.VMEM((in_dim // 128, rows * TX, 128), F32),
+            pltpu.VMEM((steps, rows, in_dim), BF16),
             pltpu.VMEM((2, TC, 2 * nb, rows, tile), F32),
             pltpu.SemaphoreType.DMA((5,)),
             pltpu.SemaphoreType.DMA((3, 1 + nb)),
@@ -371,16 +422,12 @@
         compiler_params=pltpu.CompilerParams(
             collective_id=0, has_side_effects=True, vmem_limit_bytes=60 * 1024 * 1024),
         name="recurrent",
-    )(xt, wx, wh, bias, h0, c0)
+    )(x, wx, wh, bias, h0, c0)
 
 
 def solution(mesh):
     def local_fn(x, w_in, w_rec, gate_bias, h_init, c_init):
-        rows = x.shape[0] // 2
-        row0 = (lax.axis_index("model") // 2) * rows
-        xt = lax.dynamic_slice_in_dim(x, row0, rows, 0).swapaxes(0, 1)
-        bias = jnp.pad(gate_bias, ((0, 4), (0, 0)))
-        y, h_last, c_last, _ = lstm(xt, w_in.swapaxes(0, 1), w_rec.swapaxes(0, 1), bias, h_init, c_init)
+        y, h_last, c_last, _ = lstm(x, w_in.swapaxes(0, 1), w_rec.swapaxes(0, 1), gate_bias, h_init, c_init)
         return y.swapaxes(0, 1), h_last, c_last
 
     return jax.shard_map(

time: 491 us -> 467 us (0.951)
  local copies, waits for them, and re-layouts: 57.2 us -> 32.2 us
    unnamed x10 -> x9, local copies, waits for them, and re-layouts: 46.1 us -> 32.2 us
    dynamic_slice x1 -> x0, local copies, waits for them, and re-layouts: 9.76 us -> none  [local_fn(): xt = lax.dynamic_slice_in_dim(x, row0, rows, 0).swapaxes(0, 1)]
where the time goes in v3:
time: 467 us; the launch traced here: 466 us
  Pallas kernels  434 us (93%)
  local copies, waits for them, and re-layouts  32.2 us (7%)
    pallas_call x1, Pallas kernels, lstm(): pl.pallas_call(kernel, out_shape=(jax.ShapeDtypeStruct((steps, batch, uni...  434 us
    unnamed x9, local copies, waits for them, and re-layouts  32.2 us

profile of v3, /device:TPU:0, one launch (start us, length us, event | category | flops | bytes accessed | tf_op | source)
XLA Modules:
  0.0 466.5 jit_solution(12470665240156346346)
XLA Ops:
  0.6 3.8 copy.15
  4.4 8.5 %copy.14 = bf16[2048,4,512]{2,0,1:T(8,128)(2,1)} copy(bf16[2048,4,512]{2,1,0:T(4,128)(2,1)} %param.8) | data formatting | bytes 16777216 | tf_op args[2]
  12.9 433.6 %recurrent.1 = (bf16[128,128,512]{2,1,0:T(8,128)(2,1)}, f32[128,512]{1,0:T(8,128)}, f32[128,512]{1,0:T(8,128)}, f32[128,16,64,256]{3,2,1,0:T(8,128)}) custom-call(bf16[128,128,640]{2,1,0:T(8,128)(2,1)} %refs_0_.1, bf16[4,640,512]{2,1,0:T(8,128)(2,1)} %bitcast.9, bf16[4,2048,512]{2,1,0:T(8,128)(2,1)} %bitcast.7, f32[4,512]{1,0:T(4,128)} %refs_3_.1, ...), custom_call_target="tpu_custom_call" | custom-call | tf_op jit(solution)/shard_map/recurrent/pallas_call | solution.py:388
  446.4 0.0 copy-start.1
  446.5 0.0 copy-start
  446.5 18.6 %copy.11 = bf16[128,128,512]{2,1,0:T(8,128)(2,1)} copy(bf16[128,128,512]{2,0,1:T(8,128)(2,1)} %bitcast.8) | data formatting | bytes 33554432
  465.1 0.0 copy-done.1
  465.1 0.7 copy.18
  465.8 0.0 copy-done
  465.8 0.7 copy.19
Async XLA Ops:
  446.4 18.6 %copy-start.1 = (f32[128,512]{1,0:T(8,128)S(1)}, f32[128,512]{1,0:T(8,128)}, u32[]{:S(2)}) copy-start(f32[128,512]{1,0:T(8,128)} %get-tuple-element.16) | copy-start | bytes 786436
  446.5 19.3 %copy-start = (f32[128,512]{1,0:T(8,128)S(1)}, f32[128,512]{1,0:T(8,128)}, u32[]{:S(2)}) copy-start(f32[128,512]{1,0:T(8,128)} %get-tuple-element.17) | copy-start | bytes 786436

commit v4 on v3

--- a/solution.py
+++ b/solution.py
@@ -12,7 +12,7 @@
 XSLOTS = 3
 TX = 16
 TC = 8
-LAG = 2
+LAG = 6
 DELAY = 2
 AHEAD = 5
 CH = 128

time: 467 us -> 459 us (0.983)
  Pallas kernels: 434 us -> 425 us
    pallas_call x1, Pallas kernels: 434 us -> 425 us  [lstm(): pl.pallas_call(kernel, out_shape=(jax.ShapeDtypeStruct((steps, batch, uni...]
where the time goes in v4:
time: 459 us; the launch traced here: 458 us
  Pallas kernels  425 us (93%)
  local copies, waits for them, and re-layouts  32.2 us (7%)
    pallas_call x1, Pallas kernels, lstm(): pl.pallas_call(kernel, out_shape=(jax.ShapeDtypeStruct((steps, batch, uni...  425 us
    unnamed x9, local copies, waits for them, and re-layouts  32.2 us

profile of v4, /device:TPU:0, one launch (start us, length us, event | category | flops | bytes accessed | tf_op | source)
XLA Modules:
  0.0 458.1 jit_solution(17448199368123079919)
XLA Ops:
  0.6 3.8 copy.15
  4.4 8.5 %copy.14 = bf16[2048,4,512]{2,0,1:T(8,128)(2,1)} copy(bf16[2048,4,512]{2,1,0:T(4,128)(2,1)} %param.8) | data formatting | bytes 16777216 | tf_op args[2]
  12.9 425.2 %recurrent.1 = (bf16[128,128,512]{2,1,0:T(8,128)(2,1)}, f32[128,512]{1,0:T(8,128)}, f32[128,512]{1,0:T(8,128)}, f32[128,16,64,256]{3,2,1,0:T(8,128)}) custom-call(bf16[128,128,640]{2,1,0:T(8,128)(2,1)} %refs_0_.1, bf16[4,640,512]{2,1,0:T(8,128)(2,1)} %bitcast.9, bf16[4,2048,512]{2,1,0:T(8,128)(2,1)} %bitcast.7, f32[4,512]{1,0:T(4,128)} %refs_3_.1, ...), custom_call_target="tpu_custom_call" | custom-call | tf_op jit(solution)/shard_map/recurrent/pallas_call | solution.py:388
  438.1 0.0 copy-start.1
  438.1 0.0 copy-start
  438.1 18.6 %copy.11 = bf16[128,128,512]{2,1,0:T(8,128)(2,1)} copy(bf16[128,128,512]{2,0,1:T(8,128)(2,1)} %bitcast.8) | data formatting | bytes 33554432
  456.7 0.0 copy-done.1
  456.7 0.7 copy.18
  457.4 0.0 copy-done
  457.4 0.7 copy.19
Async XLA Ops:
  438.1 18.6 %copy-start.1 = (f32[128,512]{1,0:T(8,128)S(1)}, f32[128,512]{1,0:T(8,128)}, u32[]{:S(2)}) copy-start(f32[128,512]{1,0:T(8,128)} %get-tuple-element.16) | copy-start | bytes 786436
  438.1 19.3 %copy-start = (f32[128,512]{1,0:T(8,128)S(1)}, f32[128,512]{1,0:T(8,128)}, u32[]{:S(2)}) copy-start(f32[128,512]{1,0:T(8,128)} %get-tuple-element.17) | copy-start | bytes 786436
